TPU v7x, 32 devices: a whole 2x2x4 slice. The times are simulated.
32 devices in a mesh: blk: 16 (over z, x, core), col: 2 (over y).
Axes of the slice: x: 2, y: 2, z: 4, core: 2. Of those that a mesh axis runs over, the one named last changes fastest.
Arguments:
- blocks: bfloat16 [16, 2, 2048, 2048], P('blk'), may hold values from -0.09375 to 0.09375
- offsets: int32 [16, 2], P('blk'), may hold values from -2 to 2, as said below
- krylov: bfloat16 [16, 64, 32768], P('col', None, 'blk'), may hold values from -6 to 6
- previous: float32 [64, 16, 32768], P(None, 'col', 'blk')
- node_table: float32 [32], replicated, may hold values from -1.5 to 1.5
- node_index: int32 [16], P('col'), may hold values from 0 to 31
- pole_values: float32 [16], P('col'), may hold values from 4 to 16
- scaling: float32 [16], P('col'), may hold values from 0.5 to 2
Outputs:
- new_basis: bfloat16 [16, 64, 32768], P('col', None, 'blk')
- first_coeffs: float32 [64, 64], replicated
- second_coeffs: float32 [64, 64], replicated
- factor: float32 [64, 64], replicated
Inputs may be any that keep to these rules, and one draw needn't show every extreme that they name: `offsets`: each block row's 2 distances are distinct.
All inputs are finite; a program needn't handle non-finite values.
Results may differ from a plain program's by a relative error of at most 0.0012.
Values may be sent and summed in bfloat16 or wider, within the bound.
A program may use at most 128 MiB of HBM per device.

v0:
```python
import functools
import math

import jax
import jax.numpy as jnp
from jax import lax
from jax.experimental import pallas as pl
from jax.experimental.pallas import tpu as pltpu
from jax.sharding import PartitionSpec as P

REACH = 2
WIDTH = 2 * REACH + 1
BF = jnp.bfloat16
F32 = jnp.float32
NT = (((1,), (1,)), ((), ()))
MESH = pl.DeviceIdType.MESH


def split(x):
    high = x.astype(BF)
    return high, (x - high.astype(F32)).astype(BF)


def dot_nt(a, b):
    return lax.dot_general(a, b, NT, preferred_element_type=F32)


def expand_kernel(
    n_blk, n_col, terms, cols, rows, groups,
    offsets, node_index, node_table, pole_values, scaling,
    krylov, blocks, previous,
    w_out, p_out, reduced,
    *scratch,
):
    bufs = scratch[:terms]
    (carry, band, prev, image, a_send, a_recv, b_send, b_recv, c_send, c_recv,
     d_send, d_recv, y_send, y_recv, own_sem, band_sem, prev_sem,
     wst, pst, sums, last_sum, basis_sum, part, rs_buf, z_buf, ag_buf,
     w_sem, p_sem, rs_send, rs_recv, z_send, z_recv, ag_send, ag_recv) = scratch[terms:]
    me = lax.axis_index("blk")
    col = lax.axis_index("col")
    core = lax.rem(me, 2)
    chip = lax.div(me, 2)
    par = lax.rem(chip, 2)
    n_chip = n_blk // 2
    n_prev = previous.shape[0]
    partner = (chip + 1 - 2 * par) * 2 + core
    ahead = lax.rem(chip + 2 - 4 * par + n_chip, n_chip) * 2 + core
    sibling = chip * 2 + 1 - core

    def remote(src, dst, send, recv, blk, colpos=None):
        return pltpu.make_async_remote_copy(
            src_ref=src, dst_ref=dst, send_sem=send, recv_sem=recv,
            device_id=(blk, col if colpos is None else colpos), device_id_type=MESH)

    own = [pltpu.make_async_copy(krylov.at[k], bufs[k].at[REACH], own_sem.at[k]) for k in range(terms)]
    band_copy = [pltpu.make_async_copy(blocks.at[0, c], band.at[c], band_sem.at[c]) for c in range(band.shape[0])]
    prev_copy = pltpu.make_async_copy(previous, prev, prev_sem)
    prev_copy.start()

    team, depth = part.shape[0], z_buf.shape[0]
    place = lax.rem(me, 4)
    layer = lax.div(me, 4)
    pos = place * n_col + col

    def member(j):
        other = lax.rem(pos + j, team)
        return other, layer * 4 + lax.div(other, n_col), lax.rem(other, n_col)

    def peer(j):
        return lax.rem(layer + j, depth) * 4 + place

    barrier = pltpu.get_barrier_semaphore()
    for j in range(1, team):
        _, blk, at_col = member(j)
        pl.semaphore_signal(barrier, inc=1, device_id=(blk, at_col), device_id_type=MESH)
    for j in range(1, depth):
        pl.semaphore_signal(barrier, inc=1, device_id=(peer(j), col), device_id_type=MESH)
    pl.semaphore_wait(barrier, team + depth - 2)

    a_copy = [remote(krylov.at[k], bufs[k].at[4 * par], a_send.at[k], a_recv.at[k], partner) for k in range(terms)]
    c_copy = [remote(krylov.at[k], bufs[k].at[1 + 2 * core], c_send.at[k], c_recv.at[k], sibling) for k in range(terms)]
    b_copy = [remote(bufs[k].at[4 - 4 * par], bufs[k].at[4 * par], b_send.at[k], b_recv.at[k], ahead) for k in range(terms)]
    d_copy = [remote(bufs[k].at[4 - 4 * core], bufs[k].at[3 - 2 * core], d_send.at[k], d_recv.at[k], sibling) for k in range(terms)]
    y_copy = remote(krylov.at[terms - 1], carry, y_send, y_recv, me, lax.rem(col + 1, n_col))

    for k in range(terms):
        a_copy[k].start()
    for k in range(terms):
        c_copy[k].start()
    if n_col > 1:
        @pl.when(col < n_col - 1)
        def _():
            y_copy.start()
    for k in range(terms):
        own[k].start()
    for copy in band_copy:
        copy.start()

    @pl.when(col == 0)
    def _():
        carry[...] = jnp.zeros_like(carry)

    w_copy = [pltpu.make_async_copy(wst.at[t], w_out.at[t], w_sem.at[t]) for t in range(terms)]
    p_copy = pltpu.make_async_copy(pst, p_out, p_sem)
    lane = 256

    def arrange(t):
        if t == 0:
            prev_copy.wait()
        p_at = t * 16

        def step(i, _):
            at = pl.ds(pl.multiple_of(i * lane, lane), lane)
            high, low = split(jnp.swapaxes(prev[p_at:p_at + 16, :, at], 0, 1))
            pst[:, p_at:p_at + 16, at] = high
            pst[:, n_prev + p_at:n_prev + p_at + 16, at] = low
            return 0
        lax.fori_loop(0, rows // lane, step, 0)
        if p_at + 16 == n_prev:
            p_copy.start()

    def basis_term(t):
        part = dot_nt(pst[t], pst[t, :n_prev])
        if t == 0:
            basis_sum[...] = part
        else:
            basis_sum[...] += part

    tile = 256
    n_coupling = band.shape[0]

    def ready(group):
        for t in group:
            c_copy[t].wait_recv()
            d_copy[t].wait_recv()
            own[t].wait()
        if group[0] == 0:
            for copy in band_copy:
                copy.wait()

    def image_part(group, start, count):
        picks = [
            jnp.concatenate([bufs[t][offsets[0, c] + REACH] for t in group], axis=0)
            for c in range(n_coupling)
        ]

        def step(i, _):
            at = pl.ds(pl.multiple_of(i * tile, tile), tile)
            total = dot_nt(picks[0], band[0, at, :])
            for c in range(1, n_coupling):
                total = total + dot_nt(picks[c], band[c, at, :])
            image[group[0] * cols:(group[-1] + 1) * cols, at] = total
            return 0
        lax.fori_loop(start, start + count, step, 0)

    def finish(group):
        for t in group:
            shift = jnp.full((8, 128), node_table[node_index[t]], F32)
            weight = jnp.full((8, 128), scaling[t], F32) / (
                1.0 - shift / jnp.full((8, 128), pole_values[t], F32))
            before = carry if t == 0 else bufs[t - 1].at[REACH]
            if t == 0 and n_col > 1:
                @pl.when(col > 0)
                def _():
                    y_copy.wait_recv()
            work = (
                image[t * cols:(t + 1) * cols, :]
                - shift[:1, :1] * bufs[t][REACH].astype(F32)
                + weight[:1, :1] * before[...].astype(F32)
            )
            high, low = split(work)
            wst[t, :cols] = high
            wst[t, cols:] = low
            w_copy[t].start()
            top = dot_nt(pst[t], high)
            self_part = dot_nt(wst[t], high)
            extra = dot_nt(pst[t, :n_prev], low)
            if t == 0:
                sums[:2 * n_prev] = top
                sums[2 * n_prev:] = self_part
                last_sum[...] = extra
            else:
                sums[:2 * n_prev] += top
                sums[2 * n_prev:] += self_part
                last_sum[...] += extra

    n_tiles = rows // tile
    plan = {}
    for j in range(n_prev // 16):
        plan.setdefault(j // 2, []).append(functools.partial(arrange, j))
    for t in range(terms):
        plan.setdefault(-(-n_prev // 32) + t // 3, []).append(functools.partial(basis_term, t))
    first, second, third = groups
    begin = min(terms - 1, first[-1] + 2)
    half = n_tiles // 2
    plan.setdefault(begin, []).extend([
        functools.partial(ready, first), functools.partial(image_part, first, 0, half)])
    plan.setdefault(begin + 1, []).append(functools.partial(image_part, first, half, n_tiles - half))
    plan.setdefault(begin + 2, []).extend([
        functools.partial(finish, first), functools.partial(ready, second),
        functools.partial(image_part, second, 0, half)])
    plan.setdefault(begin + 3, []).extend([
        functools.partial(image_part, second, half, n_tiles - half), functools.partial(finish, second)])

    for k in range(terms + 1):
        if k < terms:
            a_copy[k].wait_recv()
            b_copy[k].start()

            @pl.when(par == core)
            def _():
                d_copy[k].start()
        if k > 0:
            b_copy[k - 1].wait_recv()

            @pl.when(par != core)
            def _():
                d_copy[k - 1].start()
        for item in plan.get(k, ()):
            item()
    ready(third)
    image_part(third, 0, n_tiles)
    finish(third)
    low = sums[2 * n_prev + cols:]
    head = jnp.concatenate([
        sums[:n_prev] + sums[n_prev:2 * n_prev] + last_sum[...],
        sums[2 * n_prev:2 * n_prev + cols] + low + low.T,
    ], axis=1)
    low = basis_sum[n_prev:]
    basis = basis_sum[:n_prev] + low + low.T
    full = jnp.concatenate([head, jnp.concatenate([basis, jnp.zeros_like(basis)], axis=1)], axis=0)
    part[...] = full.reshape(part.shape)
    copies = []
    for j in range(1, team):
        other, blk, at_col = member(j)
        copies.append(remote(part.at[other], rs_buf.at[j - 1], rs_send.at[j - 1], rs_recv.at[j - 1], blk, at_col))
        copies[-1].start()
    total = part[pos]
    for j, copy in enumerate(copies):
        copy.wait_recv()
        total = total + rs_buf[j]
    z_buf[layer] = total
    z_copies = [
        remote(z_buf.at[layer], z_buf.at[layer], z_send.at[j - 1], z_recv.at[j - 1], peer(j))
        for j in range(1, depth)]
    for copy in z_copies:
        copy.start()
    for copy in z_copies:
        copy.wait_recv()
    total = z_buf[0]
    for j in range(1, depth):
        total = total + z_buf[j]
    ag_buf[pos] = total
    ag_copies = []
    for j in range(1, team):
        _, blk, at_col = member(j)
        ag_copies.append(remote(ag_buf.at[pos], ag_buf.at[pos], ag_send.at[j - 1], ag_recv.at[j - 1], blk, at_col))
        ag_copies[-1].start()
    for k in range(terms):
        a_copy[k].wait_send()
        b_copy[k].wait_send()
        c_copy[k].wait_send()
        d_copy[k].wait_send()
        w_copy[k].wait()
    p_copy.wait()
    if n_col > 1:
        @pl.when(col < n_col - 1)
        def _():
            y_copy.wait_send()
    for copy in ag_copies:
        copy.wait_recv()
    reduced[...] = ag_buf[...].reshape(reduced.shape)
    for copy in copies + z_copies + ag_copies:
        copy.wait_send()


def expand(n_blk, n_col, blocks, offsets, krylov, previous, node_table, node_index, pole_values, scaling):
    terms, cols, rows = krylov.shape
    n_prev = previous.shape[0]
    groups = (tuple(range(terms // 2)), tuple(range(terms // 2, 3 * terms // 4)), tuple(range(3 * terms // 4, terms)))
    smem = pl.BlockSpec(memory_space=pltpu.SMEM)
    hbm = pl.BlockSpec(memory_space=pl.ANY)
    vmem = pl.BlockSpec(memory_space=pltpu.VMEM)
    dma = pltpu.SemaphoreType.DMA
    team, depth = 4 * n_col, n_blk // 4
    height = cols + n_prev
    piece = (height // team, 2 * cols)
    return pl.pallas_call(
        functools.partial(expand_kernel, n_blk, n_col, terms, cols, rows, groups),
        out_shape=(
            jax.ShapeDtypeStruct((terms, 2 * cols, rows), BF),
            jax.ShapeDtypeStruct((terms, 2 * n_prev, rows), BF),
            jax.ShapeDtypeStruct((height, 2 * cols), F32),
        ),
        in_specs=[smem] * 5 + [hbm] * 3,
        out_specs=(hbm, hbm, vmem),
        scratch_shapes=[pltpu.VMEM((WIDTH, cols, rows), BF)] * terms + [
            pltpu.VMEM((cols, rows), BF),
            pltpu.VMEM(blocks.shape[1:], BF),
            pltpu.VMEM(previous.shape, F32),
            pltpu.VMEM((terms * cols, rows), F32),
        ] + [dma((terms,))] * 8 + [dma, dma, dma((terms,)), dma((blocks.shape[1],)), dma] + [
            pltpu.VMEM((terms, 2 * cols, rows), BF),
            pltpu.VMEM((terms, 2 * n_prev, rows), BF),
            pltpu.VMEM((2 * n_prev + 2 * cols, cols), F32),
            pltpu.VMEM((n_prev, cols), F32),
            pltpu.VMEM((2 * n_prev, n_prev), F32),
            pltpu.VMEM((team,) + piece, F32),
            pltpu.VMEM((team - 1,) + piece, F32),
            pltpu.VMEM((depth,) + piece, F32),
            pltpu.VMEM((team,) + piece, F32),
            dma((terms,)), dma,
            dma((team - 1,)), dma((team - 1,)),
            dma((depth - 1,)), dma((depth - 1,)),
            dma((team - 1,)), dma((team - 1,)),
        ],
        compiler_params=pltpu.CompilerParams(
            collective_id=0, has_side_effects=True, vmem_limit_bytes=60 * 1024 * 1024),
    )(offsets, node_index, node_table, pole_values, scaling,
      krylov, blocks, previous)


def exact(a, b):
    return jnp.dot(a, b, precision=lax.Precision.HIGHEST, preferred_element_type=F32)


def final_kernel(total_size, reduced, w_in, p_in, out, first, second, factor, stack, result, in_sem, out_sem):
    terms, depth, rows = stack.shape
    cols = first.shape[1]
    n_prev = first.shape[0]
    w_copy = [pltpu.make_async_copy(w_in.at[t], stack.at[t, pl.ds(0, 2 * cols)], in_sem.at[0, t]) for t in range(terms)]
    p_copy = [pltpu.make_async_copy(p_in.at[t], stack.at[t, pl.ds(2 * cols, 2 * n_prev)], in_sem.at[1, t]) for t in range(terms)]
    for t in range(terms):
        w_copy[t].start()
        p_copy[t].start()
    inverse_size = 1.0 / total_size
    root_size = math.sqrt(total_size)
    cross = reduced[:n_prev, :cols] * inverse_size
    self_gram = reduced[:n_prev, cols:] * inverse_size
    basis_gram = reduced[n_prev:, :n_prev] * inverse_size
    coeff_two = cross - exact(basis_gram, cross)
    combined = cross + coeff_two
    turned = combined.T
    mixed = exact(turned, cross)
    gram = self_gram - mixed - mixed.T + exact(turned, exact(basis_gram, combined))
    first[...] = cross * root_size
    second[...] = coeff_two * root_size
    row = lax.broadcasted_iota(jnp.int32, (cols, cols), 0)
    lane = lax.broadcasted_iota(jnp.int32, (cols, cols), 1)
    both = jnp.concatenate([gram, jnp.where(row == lane, 1.0, 0.0)], axis=1)
    below = lax.broadcasted_iota(jnp.int32, (cols, 1), 0)
    for k in range(cols - 1):
        ratio = jnp.where(below > k, both[:, k:k + 1] * (1.0 / both[k:k + 1, k:k + 1]), 0.0)
        both = both - ratio * both[k:k + 1, :]
    left, right = both[:, :cols], both[:, cols:]
    pivots = jnp.sum(jnp.where(row == lane, left, 0.0), axis=1, keepdims=True)
    scale = 1.0 / jnp.sqrt(pivots)
    factor[...] = jnp.where(lane >= row, left * scale, 0.0).T
    inverse = jnp.where(lane <= row, right * scale, 0.0)
    mix = -exact(inverse, turned)
    fh, fl = split(inverse)
    dh, dl = split(mix)
    zero_f, zero_d = jnp.zeros_like(fl), jnp.zeros_like(dl)
    weights = jnp.concatenate([
        jnp.concatenate([fh, fh, dh, dh], axis=1),
        jnp.concatenate([fl, zero_f, dl, zero_d], axis=1),
    ], axis=0)
    out_copy = [pltpu.make_async_copy(result.at[t], out.at[t], out_sem.at[t]) for t in range(terms)]
    for t in range(terms):
        w_copy[t].wait()
        p_copy[t].wait()
        both = jnp.dot(weights, stack[t], preferred_element_type=F32)
        result[t] = (both[:cols] + both[cols:]).astype(BF)
        out_copy[t].start()
    for t in range(terms):
        out_copy[t].wait()


def final(total_size, reduced, wst, pst):
    terms, _, rows = wst.shape
    cols, n_prev = wst.shape[1] // 2, pst.shape[1] // 2
    vmem = pl.BlockSpec(memory_space=pltpu.VMEM)
    hbm = pl.BlockSpec(memory_space=pl.ANY)
    small = jax.ShapeDtypeStruct((n_prev, cols), F32)
    dma = pltpu.SemaphoreType.DMA
    return pl.pallas_call(
        functools.partial(final_kernel, total_size),
        out_shape=(jax.ShapeDtypeStruct((terms, cols, rows), BF), small, small, jax.ShapeDtypeStruct((cols, cols), F32)),
        in_specs=[vmem, hbm, hbm],
        out_specs=(hbm, vmem, vmem, vmem),
        scratch_shapes=[
            pltpu.VMEM((terms, 2 * cols + 2 * n_prev, rows), BF),
            pltpu.VMEM((terms, cols, rows), BF),
            dma((2, terms)), dma((terms,)),
        ],
        compiler_params=pltpu.CompilerParams(vmem_limit_bytes=60 * 1024 * 1024),
    )(reduced, wst, pst)


def body(n_blk, n_col, blocks, offsets, krylov, previous, node_table, node_index, pole_values, scaling):
    terms, cols, rows = krylov.shape
    wst, pst, reduced = expand(
        n_blk, n_col, blocks, offsets, krylov, previous, node_table, node_index, pole_values, scaling)
    return final(rows * n_blk * terms * n_col, reduced, wst, pst)


def solution(mesh):
    in_specs = (
        P("blk", None, None, None),
        P("blk", None),
        P("col", None, "blk"),
        P(None, "col", "blk"),
        P(),
        P("col"),
        P("col"),
        P("col"),
    )
    out_specs = (P("col", None, "blk"), P(), P(), P())
    call = functools.partial(body, mesh.shape["blk"], mesh.shape["col"])
    return jax.shard_map(call, mesh=mesh, in_specs=in_specs, out_specs=out_specs, check_vma=False)
```

profile of v0, /device:TPU:0, one launch (start us, length us, event | category | flops | bytes accessed | tf_op | source)
XLA Modules:
  0.0 95.4 jit_solution(4892078748462173302)
XLA Ops:
  0.6 83.4 %shard_map.111 = (bf16[8,128,2048]{2,1,0:T(8,128)(2,1)}, bf16[8,128,2048]{2,1,0:T(8,128)(2,1)}, f32[128,128]{1,0:T(8,128)}) custom-call(s32[1,2]{1,0:T(1,128)} %offsets.1, s32[8]{0:T(128)} %node_index.1, f32[32]{0:T(128)} %node_table.1, f32[8]{0:T(128)} %pole_values.1, f32[8]{0:T(128)} %scaling.1, bf16[8,64,2048]{2,1,0:T(8,128)(2,1)} %krylov.1, ...), custom_call_target="tpu_custom_call" | custom-call | tf_op jit(solution)/shard_map/pallas_call | solution.py:289
  84.1 11.3 %shard_map.112 = (bf16[8,64,2048]{2,1,0:T(8,128)(2,1)}, f32[64,64]{1,0:T(8,128)}, f32[64,64]{1,0:T(8,128)}, f32[64,64]{1,0:T(8,128)}) custom-call(f32[128,128]{1,0:T(8,128)} %get-tuple-element.7.reduced, bf16[8,128,2048]{2,1,0:T(8,128)(2,1)} %get-tuple-element.8.w_in, bf16[8,128,2048]{2,1,0:T(8,128)(2,1)} %get-tuple-element.9.p_in), custom_call_target="tpu_custom_call" | custom-call | tf_op jit(solution)/shard_map/pallas_call | solution.py:387
where the time goes:
time: 95.6 us; the launch traced here: 95.4 us
  Pallas kernels  94.7 us (99%)
    pallas_call x1, Pallas kernels, expand(): pl.pallas_call(functools.partial(expand_kernel, n_blk, n_col, terms, cols...  83.4 us
    pallas_call x1, Pallas kernels, final(): pl.pallas_call(functools.partial(final_kernel, total_size), out_shape=(ja...  11.3 us

commit v1 on v0

v1 whole, which is shorter than its diff:
```python
import functools
import math

import jax
import jax.numpy as jnp
from jax import lax
from jax.experimental import pallas as pl
from jax.experimental.pallas import tpu as pltpu
from jax.sharding import PartitionSpec as P

REACH = 2
WIDTH = 2 * REACH + 1
PAIR = 2
CHUNK = 256
WINDOW = 3
LAG = 4
SENDS = 4
A_RING = 2 * WINDOW
B_SENDS = 6
D_RING = 2 * LAG + 2
BF = jnp.bfloat16
F32 = jnp.float32
NT = (((1,), (1,)), ((), ()))
MESH = pl.DeviceIdType.MESH


def split(x):
    high = x.astype(BF)
    return high, (x - high.astype(F32)).astype(BF)


def dot_nt(a, b):
    return lax.dot_general(a, b, NT, preferred_element_type=F32)


def exact(a, b):
    return jnp.dot(a, b, precision=lax.Precision.HIGHEST, preferred_element_type=F32)


def expand_kernel(
    n_blk, n_col, terms, cols, rows, total_size,
    offsets_in, node_index_in, node_table_in, pole_values_in, scaling_in,
    krylov, blocks, previous,
    wst, pst, reduced,
    offsets, node_index, node_table, pole_values, scaling, scalar_sem,
    bufs, carry, band, prev, image, sums, basis_sum,
    a_send, a_recv, b_send, b_recv, c_send, c_recv, d_send, d_recv,
    y_send, y_recv, own_sem, band_sem, prev_sem,
    part, rs_buf, z_buf, ag_buf, red_send, rs_recv, z_recv, ag_recv,
):
    me = lax.axis_index("blk")
    col = lax.axis_index("col")
    core = lax.rem(me, 2)
    chip = lax.div(me, 2)
    par = lax.rem(chip, 2)
    n_chip = n_blk // 2
    n_prev = previous.shape[0]
    partner = (chip + 1 - 2 * par) * 2 + core
    ahead = lax.rem(chip + 2 - 4 * par + n_chip, n_chip) * 2 + core
    sibling = chip * 2 + 1 - core
    per_group = rows // CHUNK
    n_group = terms // PAIR
    n_piece = n_group * per_group

    def remote(src, dst, send, recv, blk, colpos=None):
        return pltpu.make_async_remote_copy(
            src_ref=src, dst_ref=dst, send_sem=send, recv_sem=recv,
            device_id=(blk, col if colpos is None else colpos), device_id_type=MESH)

    def place_of(s):
        if isinstance(s, int):
            return s // per_group, s % per_group
        return lax.div(s, per_group), lax.rem(s, per_group)

    def cut(s):
        group, k = place_of(s)
        return pl.ds(group * PAIR, PAIR), slice(None), pl.ds(pl.multiple_of(k * CHUNK, CHUNK), CHUNK)

    def ring(s, size):
        return s % size if isinstance(s, int) else lax.rem(s, size)

    def when(test, act):
        if isinstance(test, bool):
            if test:
                act()
        else:
            pl.when(test)(act)

    def a_copy(s):
        return remote(krylov.at[cut(s)], bufs.at[(4 * par,) + cut(s)], a_send.at[ring(s, SENDS)], a_recv.at[ring(s, A_RING)], partner)

    def b_copy(s):
        return remote(bufs.at[(4 - 4 * par,) + cut(s)], bufs.at[(4 * par,) + cut(s)], b_send.at[ring(s, B_SENDS)], b_recv.at[s], ahead)

    def d_copy(s):
        return remote(bufs.at[(4 - 4 * core,) + cut(s)], bufs.at[(3 - 2 * core,) + cut(s)], d_send.at[ring(s, SENDS)], d_recv.at[ring(s, D_RING)], sibling)

    c_copy = remote(krylov, bufs.at[1 + 2 * core], c_send, c_recv, sibling)
    own_copy = pltpu.make_async_copy(krylov, bufs.at[REACH], own_sem)
    band_copy = [pltpu.make_async_copy(blocks.at[0, c], band.at[c], band_sem.at[c]) for c in range(band.shape[0])]
    prev_copy = pltpu.make_async_copy(previous, prev, prev_sem)
    y_copy = remote(krylov.at[terms - 1], carry, y_send, y_recv, me, lax.rem(col + 1, n_col))

    team, depth = part.shape[0], z_buf.shape[0]
    place = lax.rem(me, 4)
    layer = lax.div(me, 4)
    pos = place * n_col + col

    def member(j):
        other = lax.rem(pos + j, team)
        return other, layer * 4 + lax.div(other, n_col), lax.rem(other, n_col)

    def peer(j):
        return lax.rem(layer + j, depth) * 4 + place

    def spread(src_of, dst_of, recv, targets):
        return [
            remote(src_of(j), dst_of(j), red_send.at[j - 1], recv.at[j - 1], *target)
            for j, target in targets]

    mates = [(j, member(j)[1:]) for j in range(1, team)]
    peers = [(j, (peer(j), col)) for j in range(1, depth)]
    rs_copy = spread(lambda j: part.at[member(j)[0]], lambda j: rs_buf.at[j - 1], rs_recv, mates)
    z_copy = spread(lambda j: z_buf.at[layer], lambda j: z_buf.at[layer], z_recv, peers)
    ag_copy = spread(lambda j: ag_buf.at[pos], lambda j: ag_buf.at[pos], ag_recv, mates)

    scalar_copy = [
        pltpu.make_async_copy(src, dst, scalar_sem.at[i])
        for i, (src, dst) in enumerate((
            (offsets_in, offsets), (node_index_in, node_index), (node_table_in, node_table),
            (pole_values_in, pole_values), (scaling_in, scaling)))]
    prev_copy.start()
    for copy in scalar_copy:
        copy.start()
    own_copy.start()
    for copy in band_copy:
        copy.start()

    barrier = pltpu.get_barrier_semaphore()
    for j in range(1, team):
        _, blk, at_col = member(j)
        pl.semaphore_signal(barrier, inc=1, device_id=(blk, at_col), device_id_type=MESH)
    for j in range(1, depth):
        pl.semaphore_signal(barrier, inc=1, device_id=(peer(j), col), device_id_type=MESH)
    pl.semaphore_wait(barrier, team + depth - 2)

    lax.fori_loop(0, WINDOW, lambda s, _: (a_copy(s).start(), 0)[1], 0)
    if n_col > 1:
        @pl.when(col < n_col - 1)
        def _():
            y_copy.start()
    c_copy.start()

    @pl.when(col == 0)
    def _():
        carry[...] = jnp.zeros_like(carry)

    lane = 256

    def arrange(t):
        p_at = t * 16

        def step(i, _):
            at = pl.ds(pl.multiple_of(i * lane, lane), lane)
            high, low = split(jnp.swapaxes(prev[p_at:p_at + 16, :, at], 0, 1))
            pst[:, p_at:p_at + 16, at] = high
            pst[:, n_prev + p_at:n_prev + p_at + 16, at] = low
            return 0
        lax.fori_loop(0, rows // lane, step, 0)

    def basis_term(t):
        part = dot_nt(pst[t], pst[t, :n_prev])
        if t == 0:
            basis_sum[...] = part
        else:
            basis_sum[...] += part

    def local_part(t):
        shift = jnp.full((8, 128), node_table[node_index[t]], F32)
        weight = jnp.full((8, 128), scaling[t], F32) / (
            1.0 - shift / jnp.full((8, 128), pole_values[t], F32))
        if t == 0 and n_col > 1:
            @pl.when(col > 0)
            def _():
                y_copy.wait_recv()
        before = carry[...] if t == 0 else bufs[REACH, t - 1]
        image[t * cols:(t + 1) * cols, :] = (
            weight[:1, :1] * before.astype(F32) - shift[:1, :1] * bufs[REACH, t].astype(F32))

    tile = 256
    n_coupling = band.shape[0]

    def selected(r):
        some, _, k_at = cut(r)
        slots = [bufs[j, some, :, k_at].reshape(PAIR * cols, CHUNK) for j in range(WIDTH)]
        picks = []
        for c in range(n_coupling):
            pick = slots[0]
            for j in range(1, WIDTH):
                pick = jnp.where(offsets[0, c] == j - REACH, slots[j], pick)
            picks.append(pick)
        return jnp.concatenate(picks, axis=1)

    def compute(r):
        group, k = place_of(r)
        k_at = pl.ds(pl.multiple_of(k * CHUNK, CHUNK), CHUNK)
        r_at = pl.ds(pl.multiple_of(group * PAIR * cols, PAIR * cols), PAIR * cols)
        left = selected(r)

        def step(i, _):
            at = pl.ds(pl.multiple_of(i * tile, tile), tile)
            right = jnp.concatenate([band[c, at, k_at] for c in range(n_coupling)], axis=1)
            image[r_at, at] += dot_nt(left, right)
            return 0
        lax.fori_loop(0, rows // tile, step, 0, unroll=UNROLL)

    def finish(t, first=False):
        at = pl.ds(t * cols, cols) if isinstance(t, int) else pl.ds(pl.multiple_of(t * cols, cols), cols)
        high, low = split(image[at, :])
        wst[t, :cols] = high
        wst[t, cols:] = low
        sums[...] += dot_nt(jnp.concatenate([pst[t], wst[t]], axis=0), wst[t])

    def ending():
        left = selected(n_piece - 1)
        k_at = pl.ds(rows - CHUNK, CHUNK)
        first = terms - PAIR
        acc = sums[...]
        for i in range(rows // tile):
            at = pl.ds(i * tile, tile)
            right = jnp.concatenate([band[c, at, k_at] for c in range(n_coupling)], axis=1)
            total = image[first * cols:, at] + dot_nt(left, right)
            for j in range(PAIR):
                t = first + j
                high, low = split(total[j * cols:(j + 1) * cols])
                wst[t, :cols, at] = high
                wst[t, cols:, at] = low
                both = jnp.concatenate([high, low], axis=0)
                acc = acc + dot_nt(jnp.concatenate([pst[t, :, at], both], axis=0), both)
        sums[...] = acc

    def forward_a(s):
        a_copy(s).wait_recv()
        when(s >= B_SENDS, lambda: b_copy(s - B_SENDS).wait_send())
        b_copy(s).start()

        @pl.when(par == core)
        def _():
            when(s >= SENDS, lambda: d_copy(s - SENDS).wait_send())
            d_copy(s).start()
        when(s + WINDOW >= SENDS, lambda: a_copy(s + WINDOW - SENDS).wait_send())
        when(s + WINDOW < n_piece, lambda: a_copy(s + WINDOW).start())

    def forward_b(s):
        b_copy(s).wait_recv()

        @pl.when(par != core)
        def _():
            when(s >= SENDS, lambda: d_copy(s - SENDS).wait_send())
            d_copy(s).start()

    def work_on(r):
        d_copy(r).wait_recv()
        compute(r)

    sums[...] = jnp.zeros_like(sums)
    prev_copy.wait()
    for t in range(n_prev // 16):
        arrange(t)
    for copy in scalar_copy:
        copy.wait()
    own_copy.wait()
    plan = {}
    for t in range(terms):
        plan.setdefault(t // 2, []).append(functools.partial(basis_term, t))
        plan.setdefault(t // 2, []).append(functools.partial(local_part, terms - 1 - t))
    for s in range(LAG + 1):
        forward_a(s)
        for item in plan.get(s, ()):
            item()
        if s >= LAG:
            forward_b(s - LAG)

    c_copy.wait_recv()
    for copy in band_copy:
        copy.wait()

    def main(s, _):
        forward_a(s)
        forward_b(s - LAG)
        r = s - LAG - 1
        work_on(r)
        group, k = place_of(r)

        @pl.when(k == per_group - 1)
        def _():
            for j in range(PAIR):
                finish(group * PAIR + j)
        return 0
    lax.fori_loop(LAG + 1, n_piece, main, 0)
    for s in range(n_piece, n_piece + LAG):
        forward_b(s - LAG)
        work_on(s - LAG - 1)
    d_copy(n_piece - 1).wait_recv()
    ending()
    total = sums[:n_prev] + sums[n_prev:2 * n_prev]
    gram = sums[2 * n_prev:2 * n_prev + cols] + sums[2 * n_prev + cols:]
    low = basis_sum[n_prev:]
    basis = basis_sum[:n_prev] + low + low.T
    full = jnp.concatenate([
        jnp.concatenate([total[:, :cols] + total[:, cols:], gram[:, :cols] + gram[:, cols:]], axis=1),
        jnp.concatenate([basis, jnp.zeros_like(basis)], axis=1)], axis=0)
    part[...] = full.reshape(part.shape)
    for copy in rs_copy:
        copy.start()
    total = part[pos]
    for j, copy in enumerate(rs_copy):
        copy.wait_recv()
        total = total + rs_buf[j]
    z_buf[layer] = total
    for copy in rs_copy:
        copy.wait_send()
    for copy in z_copy:
        copy.start()
    for s in range(n_piece - B_SENDS, n_piece):
        if s >= n_piece + WINDOW - SENDS:
            a_copy(s).wait_send()
        b_copy(s).wait_send()
        if s >= n_piece - SENDS:
            d_copy(s).wait_send()
    c_copy.wait_send()
    if n_col > 1:
        @pl.when(col < n_col - 1)
        def _():
            y_copy.wait_send()
    for copy in z_copy:
        copy.wait_recv()
    total = z_buf[0]
    for j in range(1, depth):
        total = total + z_buf[j]
    ag_buf[pos] = total
    for copy in z_copy:
        copy.wait_send()
    for copy in ag_copy:
        copy.start()
    for copy in ag_copy:
        copy.wait_recv()
    reduced[...] = ag_buf[...].reshape(reduced.shape)
    for copy in ag_copy:
        copy.wait_send()


UNROLL = 4


def expand(n_blk, n_col, blocks, offsets, krylov, previous, node_table, node_index, pole_values, scaling):
    terms, cols, rows = krylov.shape
    n_prev = previous.shape[0]
    hbm = pl.BlockSpec(memory_space=pl.ANY)
    vmem = pl.BlockSpec(memory_space=pltpu.VMEM)
    dma = pltpu.SemaphoreType.DMA
    team, depth = 4 * n_col, n_blk // 4
    n_piece = terms // PAIR * (rows // CHUNK)
    height = n_prev + cols
    piece = (height // team, 2 * cols)
    return pl.pallas_call(
        functools.partial(expand_kernel, n_blk, n_col, terms, cols, rows, rows * n_blk * terms * n_col),
        out_shape=(
            pltpu.VMEM((terms, 2 * cols, rows), BF),
            pltpu.VMEM((terms, 2 * n_prev, rows), BF),
            pltpu.VMEM((height, 2 * cols), F32),
        ),
        in_specs=[pl.BlockSpec(memory_space=pltpu.HBM)] * 5 + [hbm] * 3,
        out_specs=(vmem,) * 3,
        scratch_shapes=[
            pltpu.SMEM(x.shape, x.dtype) for x in (offsets, node_index, node_table, pole_values, scaling)
        ] + [
            dma((5,)),
            pltpu.VMEM((WIDTH, terms, cols, rows), BF),
            pltpu.VMEM((cols, rows), BF),
            pltpu.VMEM(blocks.shape[1:], BF),
            pltpu.VMEM(previous.shape, F32),
            pltpu.VMEM((terms * cols, rows), F32),
            pltpu.VMEM((2 * n_prev + 2 * cols, 2 * cols), F32),
            pltpu.VMEM((2 * n_prev, n_prev), F32),
        ] + [dma((n,)) for n in (SENDS, A_RING, B_SENDS, n_piece)] + [dma, dma] + [dma((n,)) for n in (SENDS, D_RING)]
        + [dma, dma, dma, dma((blocks.shape[1],)), dma] + [
            pltpu.VMEM((team,) + piece, F32),
            pltpu.VMEM((team - 1,) + piece, F32),
            pltpu.VMEM((depth,) + piece, F32),
            pltpu.VMEM((team,) + piece, F32),
        ] + [dma((n - 1,)) for n in (max(team, depth), team, depth, team)],
        compiler_params=pltpu.CompilerParams(
            collective_id=0, has_side_effects=True, vmem_limit_bytes=58589184),
    )(offsets, node_index, node_table, pole_values, scaling, krylov, blocks, previous)


def eliminate(both, cols):
    below = lax.broadcasted_iota(jnp.int32, (cols, 1), 0)
    k = 0
    while k < cols:
        width = 4 if k < 3 * cols // 8 else 8
        top = k // 8 * 8
        done, rest = both[:top], both[top:]
        row_at = below[top:]
        panel = [jnp.broadcast_to(rest[:, j:j + 1], rest.shape) for j in range(k, k + width)]
        for i in range(width):
            at = k + i - top
            ratio = jnp.where(row_at > k + i, panel[i] * (1.0 / panel[i][at:at + 1]), 0.0)
            for j in range(i + 1, width):
                panel[j] = panel[j] - ratio * panel[j][at:at + 1]
            rest = rest - ratio * rest[at:at + 1]
        both = jnp.concatenate([done, rest], axis=0) if top else rest
        k += width
    return both


def final_kernel(total_size, reduced, wst, pst, out, first_out, second_out, factor_out, first, second, factor, result, out_sem, small_sem):
    terms, depth, rows = wst.shape
    cols = depth // 2
    n_prev = first.shape[0]
    inverse_size = 1.0 / total_size
    root_size = math.sqrt(total_size)
    cross = reduced[:n_prev, :cols] * inverse_size
    self_gram = reduced[:n_prev, cols:] * inverse_size
    basis_gram = reduced[n_prev:, :n_prev] * inverse_size
    turned = cross.T
    once = exact(basis_gram, cross)
    coeff_two = cross - once
    combined = cross + coeff_two
    twice = exact(basis_gram, once)
    back = combined.T
    gram = self_gram - exact(
        jnp.concatenate([turned, back], axis=1),
        jnp.concatenate([combined, coeff_two - once + twice], axis=0))
    first[...] = cross * root_size
    second[...] = coeff_two * root_size
    small_copy = [
        pltpu.make_async_copy(src, dst, small_sem.at[i])
        for i, (src, dst) in enumerate(((first, first_out), (second, second_out), (factor, factor_out)))]
    small_copy[0].start()
    small_copy[1].start()
    row = lax.broadcasted_iota(jnp.int32, (cols, cols), 0)
    lane = lax.broadcasted_iota(jnp.int32, (cols, cols), 1)
    both = jnp.concatenate([gram, jnp.where(row == lane, 1.0, 0.0)], axis=1)
    both = eliminate(both, cols)
    left, right = both[:, :cols], both[:, cols:]
    pivots = jnp.sum(jnp.where(row == lane, left, 0.0), axis=1, keepdims=True)
    scale = 1.0 / jnp.sqrt(pivots)
    inverse = jnp.where(lane <= row, right * scale, 0.0)
    mix = -exact(inverse, back)
    fh, fl = split(inverse)
    dh, dl = split(mix)
    zero_f, zero_d = jnp.zeros_like(fl), jnp.zeros_like(dl)
    weights = jnp.concatenate([
        jnp.concatenate([fh, fh, dh, dh], axis=1),
        jnp.concatenate([fl, zero_f, dl, zero_d], axis=1),
    ], axis=0)
    factor[...] = jnp.where(lane >= row, left * scale, 0.0).T
    small_copy[2].start()
    out_copy = [pltpu.make_async_copy(result.at[t], out.at[t], out_sem.at[t]) for t in range(terms)]
    for t in range(terms):
        both = jnp.dot(weights, jnp.concatenate([wst[t], pst[t]], axis=0), preferred_element_type=F32)
        result[t] = (both[:cols] + both[cols:]).astype(BF)
        out_copy[t].start()
    for copy in small_copy + out_copy:
        copy.wait()


def final(total_size, reduced, wst, pst):
    terms, _, rows = wst.shape
    cols, n_prev = wst.shape[1] // 2, pst.shape[1] // 2
    vmem = pl.BlockSpec(memory_space=pltpu.VMEM)
    hbm = pl.BlockSpec(memory_space=pl.ANY)
    shape = jax.ShapeDtypeStruct
    dma = pltpu.SemaphoreType.DMA
    return pl.pallas_call(
        functools.partial(final_kernel, total_size),
        out_shape=(shape((terms, cols, rows), BF), shape((n_prev, cols), F32), shape((n_prev, cols), F32), shape((cols, cols), F32)),
        in_specs=[vmem] * 3,
        out_specs=(hbm,) * 4,
        scratch_shapes=[
            pltpu.VMEM((n_prev, cols), F32),
            pltpu.VMEM((n_prev, cols), F32),
            pltpu.VMEM((cols, cols), F32),
            pltpu.VMEM((terms, cols, rows), BF),
            dma((terms,)), dma((3,)),
        ],
        compiler_params=pltpu.CompilerParams(vmem_limit_bytes=20 * 1024 * 1024),
    )(reduced, wst, pst)


def body(n_blk, n_col, blocks, offsets, krylov, previous, node_table, node_index, pole_values, scaling):
    terms, cols, rows = krylov.shape
    wst, pst, reduced = expand(
        n_blk, n_col, blocks, offsets, krylov, previous, node_table, node_index, pole_values, scaling)
    return final(rows * n_blk * terms * n_col, reduced, wst, pst)


def solution(mesh):
    in_specs = (
        P("blk", None, None, None),
        P("blk", None),
        P("col", None, "blk"),
        P(None, "col", "blk"),
        P(),
        P("col"),
        P("col"),
        P("col"),
    )
    out_specs = (P("col", None, "blk"), P(), P(), P())
    call = functools.partial(body, mesh.shape["blk"], mesh.shape["col"])
    return jax.shard_map(call, mesh=mesh, in_specs=in_specs, out_specs=out_specs, check_vma=False)
```

time: 95.6 us -> 77.6 us (0.81)
  Pallas kernels: 94.7 us -> 76.8 us
    pallas_call x1, Pallas kernels: 83.4 us -> 71.5 us  [expand(): pl.pallas_call(functools.partial(expand_kernel, n_blk, n_col, terms, cols...]
    pallas_call x1, Pallas kernels: 11.3 us -> 5.29 us  [final(): pl.pallas_call(functools.partial(final_kernel, total_size), out_shape=(sh...]
where the time goes in v1:
time: 77.6 us; the launch traced here: 77.4 us
  Pallas kernels  76.8 us (99%)
    pallas_call x1, Pallas kernels, expand(): pl.pallas_call(functools.partial(expand_kernel, n_blk, n_col, terms, cols...  71.5 us
    pallas_call x1, Pallas kernels, final(): pl.pallas_call(functools.partial(final_kernel, total_size), out_shape=(sh...  5.29 us

profile of v1, /device:TPU:0, one launch (start us, length us, event | category | flops | bytes accessed | tf_op | source)
XLA Modules:
  0.0 77.4 jit_solution(2326278665426967618)
XLA Ops:
  0.6 71.5 %shard_map.111 = (bf16[8,128,2048]{2,1,0:T(8,128)(2,1)S(1)}, bf16[8,128,2048]{2,1,0:T(8,128)(2,1)S(1)}, f32[128,128]{1,0:T(8,128)S(1)}) custom-call(s32[1,2]{1,0:T(1,128)} %offsets_in.1, s32[8]{0:T(128)} %node_index_in.1, f32[32]{0:T(128)} %node_table_in.1, f32[8]{0:T(128)} %pole_values_in.1, f32[8]{0:T(128)} %scaling_in.1, bf16[8,64,2048]{2,1,0:T(8,128)(2,1)} %krylov.1, ...), custom_call_target="tpu_custom_call" | custom-call | tf_op jit(solution)/shard_map/pallas_call | solution.py:366
  72.1 5.3 %shard_map.112 = (bf16[8,64,2048]{2,1,0:T(8,128)(2,1)}, f32[64,64]{1,0:T(8,128)}, f32[64,64]{1,0:T(8,128)}, f32[64,64]{1,0:T(8,128)}) custom-call(f32[128,128]{1,0:T(8,128)S(1)} %get-tuple-element.7.reduced, bf16[8,128,2048]{2,1,0:T(8,128)(2,1)S(1)} %get-tuple-element.8.wst, bf16[8,128,2048]{2,1,0:T(8,128)(2,1)S(1)} %get-tuple-element.9.pst), custom_call_target="tpu_custom_call" | custom-call | tf_op jit(solution)/shard_map/pallas_call | solution.py:477

commit v2 on v1

--- a/solution.py
+++ b/solution.py
@@ -10,14 +10,14 @@
 
 REACH = 2
 WIDTH = 2 * REACH + 1
-PAIR = 2
+GROUP = 2
 CHUNK = 256
 WINDOW = 3
 LAG = 4
 SENDS = 4
 A_RING = 2 * WINDOW
 B_SENDS = 6
-D_RING = 2 * LAG + 2
+D_RING = LAG + 6
 BF = jnp.bfloat16
 F32 = jnp.float32
 NT = (((1,), (1,)), ((), ()))
@@ -59,7 +59,7 @@
     ahead = lax.rem(chip + 2 - 4 * par + n_chip, n_chip) * 2 + core
     sibling = chip * 2 + 1 - core
     per_group = rows // CHUNK
-    n_group = terms // PAIR
+    n_group = terms // GROUP
     n_piece = n_group * per_group
 
     def remote(src, dst, send, recv, blk, colpos=None):
@@ -74,7 +74,7 @@
 
     def cut(s):
         group, k = place_of(s)
-        return pl.ds(group * PAIR, PAIR), slice(None), pl.ds(pl.multiple_of(k * CHUNK, CHUNK), CHUNK)
+        return pl.ds(group * GROUP, GROUP), slice(None), pl.ds(pl.multiple_of(k * CHUNK, CHUNK), CHUNK)
 
     def ring(s, size):
         return s % size if isinstance(s, int) else lax.rem(s, size)
@@ -87,7 +87,7 @@
             pl.when(test)(act)
 
     def a_copy(s):
-        return remote(krylov.at[cut(s)], bufs.at[(4 * par,) + cut(s)], a_send.at[ring(s, SENDS)], a_recv.at[ring(s, A_RING)], partner)
+        return remote(bufs.at[(REACH,) + cut(s)], bufs.at[(4 * par,) + cut(s)], a_send.at[ring(s, SENDS)], a_recv.at[ring(s, A_RING)], partner)
 
     def b_copy(s):
         return remote(bufs.at[(4 - 4 * par,) + cut(s)], bufs.at[(4 * par,) + cut(s)], b_send.at[ring(s, B_SENDS)], b_recv.at[s], ahead)
@@ -96,12 +96,16 @@
         return remote(bufs.at[(4 - 4 * core,) + cut(s)], bufs.at[(3 - 2 * core,) + cut(s)], d_send.at[ring(s, SENDS)], d_recv.at[ring(s, D_RING)], sibling)
 
     c_copy = remote(krylov, bufs.at[1 + 2 * core], c_send, c_recv, sibling)
-    own_copy = pltpu.make_async_copy(krylov, bufs.at[REACH], own_sem)
+    own_copy = []
+    for g in range(n_group):
+        some = pl.ds(g * GROUP, GROUP)
+        own_copy.append(pltpu.make_async_copy(krylov.at[some], bufs.at[REACH, some], own_sem.at[g]))
     band_copy = [pltpu.make_async_copy(blocks.at[0, c], band.at[c], band_sem.at[c]) for c in range(band.shape[0])]
     prev_copy = pltpu.make_async_copy(previous, prev, prev_sem)
     y_copy = remote(krylov.at[terms - 1], carry, y_send, y_recv, me, lax.rem(col + 1, n_col))
 
     team, depth = part.shape[0], z_buf.shape[0]
+    half = team // 2
     place = lax.rem(me, 4)
     layer = lax.div(me, 4)
     pos = place * n_col + col
@@ -129,11 +133,11 @@
         for i, (src, dst) in enumerate((
             (offsets_in, offsets), (node_index_in, node_index), (node_table_in, node_table),
             (pole_values_in, pole_values), (scaling_in, scaling)))]
-    prev_copy.start()
+    own_copy[0].start()
     for copy in scalar_copy:
         copy.start()
-    own_copy.start()
-    for copy in band_copy:
+    prev_copy.start()
+    for copy in own_copy[1:]:
         copy.start()
 
     barrier = pltpu.get_barrier_semaphore()
@@ -144,12 +148,15 @@
         pl.semaphore_signal(barrier, inc=1, device_id=(peer(j), col), device_id_type=MESH)
     pl.semaphore_wait(barrier, team + depth - 2)
 
+    own_copy[0].wait()
     lax.fori_loop(0, WINDOW, lambda s, _: (a_copy(s).start(), 0)[1], 0)
     if n_col > 1:
         @pl.when(col < n_col - 1)
         def _():
             y_copy.start()
     c_copy.start()
+    for copy in band_copy:
+        copy.start()
 
     @pl.when(col == 0)
     def _():
@@ -192,7 +199,7 @@
 
     def selected(r):
         some, _, k_at = cut(r)
-        slots = [bufs[j, some, :, k_at].reshape(PAIR * cols, CHUNK) for j in range(WIDTH)]
+        slots = [bufs[j, some, :, k_at].reshape(GROUP * cols, k_at.size) for j in range(WIDTH)]
         picks = []
         for c in range(n_coupling):
             pick = slots[0]
@@ -201,44 +208,28 @@
             picks.append(pick)
         return jnp.concatenate(picks, axis=1)
 
+    def weights_at(at, k_at):
+        return jnp.concatenate([band[c, at, k_at] for c in range(n_coupling)], axis=1)
+
     def compute(r):
-        group, k = place_of(r)
-        k_at = pl.ds(pl.multiple_of(k * CHUNK, CHUNK), CHUNK)
-        r_at = pl.ds(pl.multiple_of(group * PAIR * cols, PAIR * cols), PAIR * cols)
+        some, _, k_at = cut(r)
+        first = some.start * cols
+        r_at = pl.ds(first if isinstance(r, int) else pl.multiple_of(first, GROUP * cols), GROUP * cols)
         left = selected(r)
 
         def step(i, _):
             at = pl.ds(pl.multiple_of(i * tile, tile), tile)
-            right = jnp.concatenate([band[c, at, k_at] for c in range(n_coupling)], axis=1)
-            image[r_at, at] += dot_nt(left, right)
+            image[r_at, at] += dot_nt(left, weights_at(at, k_at))
             return 0
         lax.fori_loop(0, rows // tile, step, 0, unroll=UNROLL)
 
-    def finish(t, first=False):
+    def finish(t):
         at = pl.ds(t * cols, cols) if isinstance(t, int) else pl.ds(pl.multiple_of(t * cols, cols), cols)
         high, low = split(image[at, :])
         wst[t, :cols] = high
         wst[t, cols:] = low
         sums[...] += dot_nt(jnp.concatenate([pst[t], wst[t]], axis=0), wst[t])
 
-    def ending():
-        left = selected(n_piece - 1)
-        k_at = pl.ds(rows - CHUNK, CHUNK)
-        first = terms - PAIR
-        acc = sums[...]
-        for i in range(rows // tile):
-            at = pl.ds(i * tile, tile)
-            right = jnp.concatenate([band[c, at, k_at] for c in range(n_coupling)], axis=1)
-            total = image[first * cols:, at] + dot_nt(left, right)
-            for j in range(PAIR):
-                t = first + j
-                high, low = split(total[j * cols:(j + 1) * cols])
-                wst[t, :cols, at] = high
-                wst[t, cols:, at] = low
-                both = jnp.concatenate([high, low], axis=0)
-                acc = acc + dot_nt(jnp.concatenate([pst[t, :, at], both], axis=0), both)
-        sums[...] = acc
-
     def forward_a(s):
         a_copy(s).wait_recv()
         when(s >= B_SENDS, lambda: b_copy(s - B_SENDS).wait_send())
@@ -267,50 +258,49 @@
     prev_copy.wait()
     for t in range(n_prev // 16):
         arrange(t)
-    for copy in scalar_copy:
+    for copy in scalar_copy + own_copy[1:]:
         copy.wait()
-    own_copy.wait()
     plan = {}
     for t in range(terms):
-        plan.setdefault(t // 2, []).append(functools.partial(basis_term, t))
-        plan.setdefault(t // 2, []).append(functools.partial(local_part, terms - 1 - t))
+        at = t * (LAG + 1) // terms
+        plan.setdefault(at, []).append(functools.partial(basis_term, t))
+        plan.setdefault(at, []).append(functools.partial(local_part, terms - 1 - t))
     for s in range(LAG + 1):
         forward_a(s)
         for item in plan.get(s, ()):
             item()
         if s >= LAG:
             forward_b(s - LAG)
-
+    low = basis_sum[n_prev:]
+    basis = basis_sum[:n_prev] + low + low.T
+    part[half:] = jnp.concatenate([basis, jnp.zeros_like(basis)], axis=1).reshape(half, *part.shape[1:])
     c_copy.wait_recv()
     for copy in band_copy:
         copy.wait()
 
     def main(s, _):
-        forward_a(s)
-        forward_b(s - LAG)
-        r = s - LAG - 1
-        work_on(r)
+        @pl.when(s < n_piece)
+        def _():
+            forward_a(s)
+        r = s - LAG - 2
+        @pl.when(r >= 0)
+        def _():
+            work_on(r)
         group, k = place_of(r)
 
-        @pl.when(k == per_group - 1)
-        def _():
-            for j in range(PAIR):
-                finish(group * PAIR + j)
+        @pl.when((r >= 0) & (k == per_group - 1))
+        def _():
+            for j in range(GROUP):
+                finish(group * GROUP + j)
+        @pl.when(s < n_piece + LAG)
+        def _():
+            forward_b(s - LAG)
         return 0
-    lax.fori_loop(LAG + 1, n_piece, main, 0)
-    for s in range(n_piece, n_piece + LAG):
-        forward_b(s - LAG)
-        work_on(s - LAG - 1)
-    d_copy(n_piece - 1).wait_recv()
-    ending()
+    lax.fori_loop(LAG + 1, n_piece + LAG + 2, main, 0)
     total = sums[:n_prev] + sums[n_prev:2 * n_prev]
     gram = sums[2 * n_prev:2 * n_prev + cols] + sums[2 * n_prev + cols:]
-    low = basis_sum[n_prev:]
-    basis = basis_sum[:n_prev] + low + low.T
-    full = jnp.concatenate([
-        jnp.concatenate([total[:, :cols] + total[:, cols:], gram[:, :cols] + gram[:, cols:]], axis=1),
-        jnp.concatenate([basis, jnp.zeros_like(basis)], axis=1)], axis=0)
-    part[...] = full.reshape(part.shape)
+    full = jnp.concatenate([total[:, :cols] + total[:, cols:], gram[:, :cols] + gram[:, cols:]], axis=1)
+    part[:half] = full.reshape(half, *part.shape[1:])
     for copy in rs_copy:
         copy.start()
     total = part[pos]
@@ -350,7 +340,7 @@
         copy.wait_send()
 
 
-UNROLL = 4
+UNROLL = 8
 
 
 def expand(n_blk, n_col, blocks, offsets, krylov, previous, node_table, node_index, pole_values, scaling):
@@ -360,7 +350,8 @@
     vmem = pl.BlockSpec(memory_space=pltpu.VMEM)
     dma = pltpu.SemaphoreType.DMA
     team, depth = 4 * n_col, n_blk // 4
-    n_piece = terms // PAIR * (rows // CHUNK)
+    n_group = terms // GROUP
+    n_piece = n_group * (rows // CHUNK)
     height = n_prev + cols
     piece = (height // team, 2 * cols)
     return pl.pallas_call(
@@ -384,7 +375,7 @@
             pltpu.VMEM((2 * n_prev + 2 * cols, 2 * cols), F32),
             pltpu.VMEM((2 * n_prev, n_prev), F32),
         ] + [dma((n,)) for n in (SENDS, A_RING, B_SENDS, n_piece)] + [dma, dma] + [dma((n,)) for n in (SENDS, D_RING)]
-        + [dma, dma, dma, dma((blocks.shape[1],)), dma] + [
+        + [dma, dma, dma((n_group,)), dma((blocks.shape[1],)), dma] + [
             pltpu.VMEM((team,) + piece, F32),
             pltpu.VMEM((team - 1,) + piece, F32),
             pltpu.VMEM((depth,) + piece, F32),

time: 77.6 us -> 76.5 us (0.986)
  Pallas kernels: 76.8 us -> 75.7 us
    pallas_call x1, Pallas kernels: 71.5 us -> 70.4 us  [expand(): pl.pallas_call(functools.partial(expand_kernel, n_blk, n_col, terms, cols...]
where the time goes in v2:
time: 76.5 us; the launch traced here: 76.4 us
  Pallas kernels  75.7 us (99%)
    pallas_call x1, Pallas kernels, expand(): pl.pallas_call(functools.partial(expand_kernel, n_blk, n_col, terms, cols...  70.4 us
    pallas_call x1, Pallas kernels, final(): pl.pallas_call(functools.partial(final_kernel, total_size), out_shape=(sh...  5.29 us

profile of v2, /device:TPU:0, one launch (start us, length us, event | category | flops | bytes accessed | tf_op | source)
XLA Modules:
  0.0 76.4 jit_solution(5573689184081858128)
XLA Ops:
  0.6 70.4 %shard_map.111 = (bf16[8,128,2048]{2,1,0:T(8,128)(2,1)S(1)}, bf16[8,128,2048]{2,1,0:T(8,128)(2,1)S(1)}, f32[128,128]{1,0:T(8,128)S(1)}) custom-call(s32[1,2]{1,0:T(1,128)} %offsets_in.1, s32[8]{0:T(128)} %node_index_in.1, f32[32]{0:T(128)} %node_table_in.1, f32[8]{0:T(128)} %pole_values_in.1, f32[8]{0:T(128)} %scaling_in.1, bf16[8,64,2048]{2,1,0:T(8,128)(2,1)} %krylov.1, ...), custom_call_target="tpu_custom_call" | custom-call | tf_op jit(solution)/shard_map/pallas_call | solution.py:357
  71.1 5.3 %shard_map.112 = (bf16[8,64,2048]{2,1,0:T(8,128)(2,1)}, f32[64,64]{1,0:T(8,128)}, f32[64,64]{1,0:T(8,128)}, f32[64,64]{1,0:T(8,128)}) custom-call(f32[128,128]{1,0:T(8,128)S(1)} %get-tuple-element.7.reduced, bf16[8,128,2048]{2,1,0:T(8,128)(2,1)S(1)} %get-tuple-element.8.wst, bf16[8,128,2048]{2,1,0:T(8,128)(2,1)S(1)} %get-tuple-element.9.pst), custom_call_target="tpu_custom_call" | custom-call | tf_op jit(solution)/shard_map/pallas_call | solution.py:468

commit v3 on v2

--- a/solution.py
+++ b/solution.py
@@ -13,11 +13,11 @@
 GROUP = 2
 CHUNK = 256
 WINDOW = 3
-LAG = 4
+LAG = 3
 SENDS = 4
-A_RING = 2 * WINDOW
+A_RING = 2 * WINDOW + 1
 B_SENDS = 6
-D_RING = LAG + 6
+D_RING = LAG + 7
 BF = jnp.bfloat16
 F32 = jnp.float32
 NT = (((1,), (1,)), ((), ()))
@@ -42,10 +42,10 @@
     offsets_in, node_index_in, node_table_in, pole_values_in, scaling_in,
     krylov, blocks, previous,
     wst, pst, reduced,
-    offsets, node_index, node_table, pole_values, scaling, scalar_sem,
+    offsets, node_index, node_table, pole_values, scaling,
     bufs, carry, band, prev, image, sums, basis_sum,
     a_send, a_recv, b_send, b_recv, c_send, c_recv, d_send, d_recv,
-    y_send, y_recv, own_sem, band_sem, prev_sem,
+    y_send, y_recv, own_sem, band_sem,
     part, rs_buf, z_buf, ag_buf, red_send, rs_recv, z_recv, ag_recv,
 ):
     me = lax.axis_index("blk")
@@ -73,6 +73,9 @@
         return lax.div(s, per_group), lax.rem(s, per_group)
 
     def cut(s):
+        if isinstance(s, int) and s >= n_piece - 1:
+            start = rows - CHUNK + (s - n_piece + 1) * (CHUNK // 2)
+            return pl.ds(terms - GROUP, GROUP), slice(None), pl.ds(start, CHUNK // 2)
         group, k = place_of(s)
         return pl.ds(group * GROUP, GROUP), slice(None), pl.ds(pl.multiple_of(k * CHUNK, CHUNK), CHUNK)
 
@@ -101,7 +104,7 @@
         some = pl.ds(g * GROUP, GROUP)
         own_copy.append(pltpu.make_async_copy(krylov.at[some], bufs.at[REACH, some], own_sem.at[g]))
     band_copy = [pltpu.make_async_copy(blocks.at[0, c], band.at[c], band_sem.at[c]) for c in range(band.shape[0])]
-    prev_copy = pltpu.make_async_copy(previous, prev, prev_sem)
+    prev_copy = pltpu.make_async_copy(previous, prev, red_send.at[5])
     y_copy = remote(krylov.at[terms - 1], carry, y_send, y_recv, me, lax.rem(col + 1, n_col))
 
     team, depth = part.shape[0], z_buf.shape[0]
@@ -129,7 +132,7 @@
     ag_copy = spread(lambda j: ag_buf.at[pos], lambda j: ag_buf.at[pos], ag_recv, mates)
 
     scalar_copy = [
-        pltpu.make_async_copy(src, dst, scalar_sem.at[i])
+        pltpu.make_async_copy(src, dst, red_send.at[i])
         for i, (src, dst) in enumerate((
             (offsets_in, offsets), (node_index_in, node_index), (node_table_in, node_table),
             (pole_values_in, pole_values), (scaling_in, scaling)))]
@@ -239,8 +242,10 @@
         def _():
             when(s >= SENDS, lambda: d_copy(s - SENDS).wait_send())
             d_copy(s).start()
-        when(s + WINDOW >= SENDS, lambda: a_copy(s + WINDOW - SENDS).wait_send())
-        when(s + WINDOW < n_piece, lambda: a_copy(s + WINDOW).start())
+
+    def refill(s):
+        when(s >= SENDS, lambda: a_copy(s - SENDS).wait_send())
+        a_copy(s).start()
 
     def forward_b(s):
         b_copy(s).wait_recv()
@@ -249,10 +254,6 @@
         def _():
             when(s >= SENDS, lambda: d_copy(s - SENDS).wait_send())
             d_copy(s).start()
-
-    def work_on(r):
-        d_copy(r).wait_recv()
-        compute(r)
 
     sums[...] = jnp.zeros_like(sums)
     prev_copy.wait()
@@ -267,6 +268,7 @@
         plan.setdefault(at, []).append(functools.partial(local_part, terms - 1 - t))
     for s in range(LAG + 1):
         forward_a(s)
+        refill(s + WINDOW)
         for item in plan.get(s, ()):
             item()
         if s >= LAG:
@@ -278,23 +280,55 @@
     for copy in band_copy:
         copy.wait()
 
+    last = n_piece - 1
+
     def main(s, _):
-        @pl.when(s < n_piece)
+        @pl.when(s < last)
         def _():
             forward_a(s)
+
+        @pl.when(s == last)
+        def _():
+            forward_a(last)
+
+        @pl.when(s + WINDOW < last)
+        def _():
+            refill(s + WINDOW)
+
+        @pl.when(s + WINDOW == last)
+        def _():
+            refill(last)
+            refill(last + 1)
         r = s - LAG - 2
         @pl.when(r >= 0)
         def _():
-            work_on(r)
+            @pl.when(r < last)
+            def _():
+                d_copy(r).wait_recv()
+
+            @pl.when(r == last)
+            def _():
+                d_copy(last).wait_recv()
+                d_copy(last + 1).wait_recv()
+            compute(r)
         group, k = place_of(r)
 
         @pl.when((r >= 0) & (k == per_group - 1))
         def _():
             for j in range(GROUP):
                 finish(group * GROUP + j)
-        @pl.when(s < n_piece + LAG)
+        @pl.when(s == last)
+        def _():
+            forward_a(last + 1)
+
+        @pl.when(s < last + LAG)
         def _():
             forward_b(s - LAG)
+
+        @pl.when(s == last + LAG)
+        def _():
+            forward_b(last)
+            forward_b(last + 1)
         return 0
     lax.fori_loop(LAG + 1, n_piece + LAG + 2, main, 0)
     total = sums[:n_prev] + sums[n_prev:2 * n_prev]
@@ -312,11 +346,11 @@
         copy.wait_send()
     for copy in z_copy:
         copy.start()
-    for s in range(n_piece - B_SENDS, n_piece):
-        if s >= n_piece + WINDOW - SENDS:
+    for s in range(n_piece + 1 - B_SENDS, n_piece + 1):
+        if s >= n_piece + 1 - SENDS:
             a_copy(s).wait_send()
         b_copy(s).wait_send()
-        if s >= n_piece - SENDS:
+        if s >= n_piece + 1 - SENDS:
             d_copy(s).wait_send()
     c_copy.wait_send()
     if n_col > 1:
@@ -366,7 +400,6 @@
         scratch_shapes=[
             pltpu.SMEM(x.shape, x.dtype) for x in (offsets, node_index, node_table, pole_values, scaling)
         ] + [
-            dma((5,)),
             pltpu.VMEM((WIDTH, terms, cols, rows), BF),
             pltpu.VMEM((cols, rows), BF),
             pltpu.VMEM(blocks.shape[1:], BF),
@@ -374,8 +407,8 @@
             pltpu.VMEM((terms * cols, rows), F32),
             pltpu.VMEM((2 * n_prev + 2 * cols, 2 * cols), F32),
             pltpu.VMEM((2 * n_prev, n_prev), F32),
-        ] + [dma((n,)) for n in (SENDS, A_RING, B_SENDS, n_piece)] + [dma, dma] + [dma((n,)) for n in (SENDS, D_RING)]
-        + [dma, dma, dma((n_group,)), dma((blocks.shape[1],)), dma] + [
+        ] + [dma((n,)) for n in (SENDS, A_RING, B_SENDS, n_piece + 1)] + [dma, dma] + [dma((n,)) for n in (SENDS, D_RING)]
+        + [dma, dma, dma((n_group,)), dma((blocks.shape[1],))] + [
             pltpu.VMEM((team,) + piece, F32),
             pltpu.VMEM((team - 1,) + piece, F32),
             pltpu.VMEM((depth,) + piece, F32),
@@ -390,7 +423,7 @@
     below = lax.broadcasted_iota(jnp.int32, (cols, 1), 0)
     k = 0
     while k < cols:
-        width = 4 if k < 3 * cols // 8 else 8
+        width = 8 if k < 3 * cols // 4 else 16
         top = k // 8 * 8
         done, rest = both[:top], both[top:]
         row_at = below[top:]

time: 76.5 us -> 76.1 us (level)
  no operation moved by 1% of the time
where the time goes in v3:
time: 76.1 us; the launch traced here: 75.9 us
  Pallas kernels  75.3 us (99%)
    pallas_call x1, Pallas kernels, expand(): pl.pallas_call(functools.partial(expand_kernel, n_blk, n_col, terms, cols...  70.3 us
    pallas_call x1, Pallas kernels, final(): pl.pallas_call(functools.partial(final_kernel, total_size), out_shape=(sh...  4.95 us

profile of v3, /device:TPU:0, one launch (start us, length us, event | category | flops | bytes accessed | tf_op | source)
XLA Modules:
  0.0 75.9 jit_solution(17853190552373871087)
XLA Ops:
  0.6 70.3 %shard_map.111 = (bf16[8,128,2048]{2,1,0:T(8,128)(2,1)S(1)}, bf16[8,128,2048]{2,1,0:T(8,128)(2,1)S(1)}, f32[128,128]{1,0:T(8,128)S(1)}) custom-call(s32[1,2]{1,0:T(1,128)} %offsets_in.1, s32[8]{0:T(128)} %node_index_in.1, f32[32]{0:T(128)} %node_table_in.1, f32[8]{0:T(128)} %pole_values_in.1, f32[8]{0:T(128)} %scaling_in.1, bf16[8,64,2048]{2,1,0:T(8,128)(2,1)} %krylov.1, ...), custom_call_target="tpu_custom_call" | custom-call | tf_op jit(solution)/shard_map/pallas_call | solution.py:391
  71.0 5.0 %shard_map.112 = (bf16[8,64,2048]{2,1,0:T(8,128)(2,1)}, f32[64,64]{1,0:T(8,128)}, f32[64,64]{1,0:T(8,128)}, f32[64,64]{1,0:T(8,128)}) custom-call(f32[128,128]{1,0:T(8,128)S(1)} %get-tuple-element.7.reduced, bf16[8,128,2048]{2,1,0:T(8,128)(2,1)S(1)} %get-tuple-element.8.wst, bf16[8,128,2048]{2,1,0:T(8,128)(2,1)S(1)} %get-tuple-element.9.pst), custom_call_target="tpu_custom_call" | custom-call | tf_op jit(solution)/shard_map/pallas_call | solution.py:501
